TPU v7x, 32 devices: a whole 2x2x4 slice. The times are simulated.
32 devices in a mesh: blk: 8 (over y, x, core), walk: 4 (over z).
Axes of the slice: x: 2, y: 2, z: 4, core: 2. Of those that a mesh axis runs over, the one named last changes fastest.
Arguments:
- walker_m: bfloat16 [4, 8, 128, 128], P('walk', 'blk'), may hold values from -6 to 6
- vertex_times: int32 [4, 8, 128], P('walk', 'blk'), may hold values from 0 to 1023
- vertex_labels: int32 [4, 8, 128], P('walk', 'blk'), may hold values from 0 to 35
- freq_index: int32 [24], replicated, may hold values from -64 to 63
- q_index: int32 [8], P('blk'), may hold values from 0 to 35
Outputs:
- g4: float32 [8, 2, 864, 864], P('blk', None, 'walk')
Inputs may be any that keep to these rules, and one draw needn't show every extreme that they name: `q_index`: entry b is 6 qx + qy for the transfer momentum (qx, qy). `freq_index`: frequency f is pi (2 n + 1) / beta with n its entry. `vertex_times`: the time is entry * beta / 1024. `vertex_labels`: site s lies at row s // 6 and column s mod 6 of the 6×6 cluster.
All inputs are finite; a program needn't handle non-finite values.
Results may differ from a plain program's by a relative error of at most 0.0061.
Values may be sent and summed in bfloat16 or wider, within the bound.
A program may use at most 128 MiB of HBM per device.

v0:
```python
import functools
import math

import jax
import jax.numpy as jnp
from jax import lax
from jax.experimental import pallas as pl
from jax.experimental.pallas import tpu as pltpu
from jax.sharding import PartitionSpec as P

SIDE = 6
TGRID = 1024
OFFSETS = (0, 1, -1, 2)
FORWARD = (2, 3, 4)


def sine(units):
    wrapped = ((units + 1024) & 2047) - 1024
    folded = jnp.where(wrapped > 512, 1024 - wrapped, wrapped)
    folded = jnp.where(wrapped < -512, -1024 - wrapped, folded)
    x = folded.astype(jnp.float32) * (math.pi / 1024.0)
    y = x * x
    total = jnp.full_like(y, 1.0 / math.factorial(13))
    for order in (11, 9, 7, 5, 3, 1):
        sign = -1.0 if (order // 2) % 2 else 1.0
        total = total * y + sign / math.factorial(order)
    return total * x


def sixth_turn(m):
    r = m - 6 * ((m * 10923) >> 16)
    half = jnp.where((r == 1) | (r == 5), 0.5, -0.5)
    cosine = jnp.where(r == 0, 1.0, jnp.where(r == 3, -1.0, half))
    root = math.sqrt(3.0) / 2.0
    side = jnp.where(r < 3, root, -root)
    return cosine.astype(jnp.float32), jnp.where((r == 0) | (r == 3), 0.0, side).astype(jnp.float32)


def visits(groups):
    around = sorted(range(1, groups), key=lambda z: min(z, groups - z))
    near = [(0, d) for d in range(len(OFFSETS))]
    far = [(z, 0) for z in around]
    return near + far + [(z, d) for z in around for d in range(1, len(OFFSETS))]


def kernel(
    groups, owners, m_in, t_in, l_in, freq_ref, q_ref, out_ref,
    m_ref, t_ref, l_ref, send_sem, recv_sem,
    odd, turn_c, turn_s, both, table, moved, left_a, left_b, left_c, right_b,
):
    order = visits(groups)
    walkers = len(order)
    w = lax.axis_index("walk")
    b = lax.axis_index("blk")

    def to_walk(z):
        return {"walk": lax.rem(w + groups - z, groups)}

    def to_blk(d):
        return {"blk": lax.rem(b + owners - OFFSETS[d], owners)}

    def copies(sources, slot, device):
        return [
            pltpu.make_async_remote_copy(
                src_ref=source,
                dst_ref=held.at[slot],
                send_sem=send_sem.at[kind, slot],
                recv_sem=recv_sem.at[kind, slot],
                device_id=device,
                device_id_type=pl.DeviceIdType.MESH,
            )
            for kind, (source, held) in enumerate(zip(sources, (m_ref, t_ref, l_ref)))
        ]

    own = (m_in.at[0, 0], t_in.at[0], l_in.at[0])

    def held_at(slot):
        return (m_ref.at[slot], t_ref.at[slot], l_ref.at[slot])

    def arrived(slot):
        for copy in copies(held_at(slot), slot, to_walk(1)):
            copy.wait_recv()

    barrier = pltpu.get_barrier_semaphore()
    peers = [{"walk": lax.rem(w + z, groups)} for z in range(1, groups)]
    reach = sorted({d % owners for d in OFFSETS + tuple(-d for d in OFFSETS)} - {0})
    peers += [{"blk": lax.rem(b + d, owners)} for d in reach]
    for peer in peers:
        pl.semaphore_signal(barrier, inc=1, device_id=peer, device_id_type=pl.DeviceIdType.MESH)
    m_ref[0] = m_in[0, 0]
    t_ref[0] = t_in[0]
    l_ref[0] = l_in[0]
    both[...] = jnp.zeros_like(both)
    out_ref[...] = jnp.zeros_like(out_ref)
    pl.semaphore_wait(barrier, len(peers))
    for z, d in [o for o in order if o[0] and not o[1]] + [o for o in order if o[1] and not o[0]]:
        for copy in copies(own, order.index((z, d)), to_walk(z) if z else to_blk(d)):
            copy.start()

    def forward(z):
        slot = order.index((z, 0))
        arrived(slot)
        for d in range(1, len(OFFSETS)):
            for copy in copies(held_at(slot), order.index((z, d)), to_blk(d)):
                copy.start()


    nf = freq_ref.shape[0]
    v = m_ref.shape[-1]
    nk = SIDE * SIDE
    own_k = out_ref.shape[2] // nf
    cols = out_ref.shape[3]
    first_k = w * own_k

    row = lax.broadcasted_iota(jnp.int32, (nf, v), 0)
    freq = jnp.zeros((nf, v), jnp.int32)
    for f in range(nf):
        freq = jnp.where(row == f, 2 * freq_ref[f] + 1, freq)
    odd[...] = freq
    q = q_ref[0]
    qx = (q * 43) >> 8
    qy = q - SIDE * qx

    scale = 1.0 / (v * v * walkers)

    def step(visit, carry):
        swap = (lax.rem(b, 2) == 1) & ((visit == 1) | (visit == 2))
        i = jnp.where(swap, 3 - visit, visit)
        for turn, z in enumerate([z for z, d in order if z and not d]):
            @pl.when(visit == FORWARD[min(turn, len(FORWARD) - 1)])
            def _(z=z):
                forward(z)

        first_far = order.index((0, len(OFFSETS) - 1)) + 1
        last_far = first_far + groups - 1

        @pl.when(((visit > 0) & (visit < first_far)) | (visit >= last_far))
        def _():
            arrived(i)

        matrix = m_ref[i]
        both[0:v, 0:v] = matrix
        both[v : 2 * v, v : 2 * v] = matrix
        times = t_ref[i]
        labels = l_ref[i]
        sx = (labels * 43) >> 8
        sy = labels - SIDE * sx
        k = lax.broadcasted_iota(jnp.int32, turn_c.shape, 0)
        kx = (k * 43) >> 8
        ky = k - SIDE * kx
        cosines, sines = sixth_turn(kx * sx + ky * sy)
        turn_c[...] = cosines
        turn_s[...] = sines
        cq, sq = sixth_turn(qx * sx + qy * sy)

        units = (odd[...] * times) & 2047
        ca = sine(units + 512)
        sa = sine(units)
        ca_q = ca * cq + sa * sq
        sa_q = sa * cq - ca * sq

        def turned(c, s, k):
            cb = turn_c[pl.ds(k, 1)]
            sb = turn_s[pl.ds(k, 1)]
            return c * cb + s * sb, s * cb - c * sb

        def put(ref, place, first, second, lanes):
            rows = slice(2 * nf * place, 2 * nf * (place + 1))
            ref[rows, lanes] = jnp.concatenate([first, second], axis=0).astype(jnp.bfloat16)

        low, high = slice(0, v), slice(v, 2 * v)
        for pair in range(nk // 2):
            c0, s0 = turned(ca, sa, 2 * pair)
            c1, s1 = turned(ca, sa, 2 * pair + 1)
            put(table, pair, c0, c1, low)
            put(table, pair, s0, s1, high)
            c0, s0 = turned(ca_q, sa_q, 2 * pair)
            c1, s1 = turned(ca_q, sa_q, 2 * pair + 1)
            put(moved, pair, c0, c1, low)
            put(moved, pair, s0, s1, high)
        for j in range(own_k):
            c, s = turned(ca, sa, first_k + j)
            put(left_b, j, c, -s, low)
            put(left_b, j, s, c, high)
            c, s = turned(ca_q, sa_q, first_k + j)
            put(left_c, j, c, s, low)
            put(left_c, j, s, -c, high)

        right_b[...] = jnp.dot(
            table[...], both[...], preferred_element_type=jnp.float32
        ).astype(jnp.bfloat16)
        product = jnp.dot(left_c[...], both[...], preferred_element_type=jnp.float32)
        left_a[...] = (product.astype(jnp.bfloat16).astype(jnp.float32) * scale).astype(jnp.bfloat16)

        contract = (((1,), (1,)), ((), ()))
        for start in range(0, cols, 256):
            stop = min(start + 256, cols)
            shifted = lax.dot_general(
                left_a[...], moved[start:stop], contract, preferred_element_type=jnp.float32
            )
            flipped = lax.dot_general(
                left_b[...], right_b[start:stop], contract, preferred_element_type=jnp.float32
            )
            for j in range(own_k):
                re = slice(2 * nf * j, 2 * nf * j + nf)
                im = slice(2 * nf * j + nf, 2 * nf * (j + 1))
                rows = slice(nf * j, nf * (j + 1))
                out_ref[0, 0, rows, start:stop] += (
                    shifted[re] * flipped[re] - shifted[im] * flipped[im]
                )
                out_ref[0, 1, rows, start:stop] += (
                    shifted[re] * flipped[im] + shifted[im] * flipped[re]
                )
        return carry

    lax.fori_loop(0, walkers, step, 0)
    for slot in range(1, walkers):
        for copy in copies(held_at(slot), slot, to_walk(1)):
            copy.wait_send()


def local(walker_m, vertex_times, vertex_labels, freq_index, q_index):
    groups = lax.axis_size("walk")
    owners = lax.axis_size("blk")
    v = walker_m.shape[-1]
    nf = freq_index.shape[0]
    k = SIDE * SIDE * nf
    own = k // groups
    walkers = groups * len(OFFSETS)
    vmem = pl.BlockSpec(memory_space=pltpu.VMEM)
    smem = pl.BlockSpec(memory_space=pltpu.SMEM)
    bf16 = jnp.bfloat16
    return pl.pallas_call(
        functools.partial(kernel, groups, owners),
        out_shape=pltpu.VMEM((1, 2, own, k), jnp.float32),
        in_specs=[vmem, vmem, vmem, smem, smem],
        out_specs=vmem,
        scratch_shapes=[
            pltpu.VMEM((walkers, v, v), bf16),
            pltpu.VMEM((walkers, 1, v), jnp.int32),
            pltpu.VMEM((walkers, 1, v), jnp.int32),
            pltpu.SemaphoreType.DMA((3, walkers)),
            pltpu.SemaphoreType.DMA((3, walkers)),
            pltpu.VMEM((nf, v), jnp.int32),
            pltpu.VMEM((40, v), jnp.float32),
            pltpu.VMEM((40, v), jnp.float32),
            pltpu.VMEM((2 * v, 2 * v), bf16),
            pltpu.VMEM((k, 2 * v), bf16),
            pltpu.VMEM((k, 2 * v), bf16),
            pltpu.VMEM((2 * own, 2 * v), bf16),
            pltpu.VMEM((2 * own, 2 * v), bf16),
            pltpu.VMEM((2 * own, 2 * v), bf16),
            pltpu.VMEM((k, 2 * v), bf16),
        ],
        compiler_params=pltpu.CompilerParams(collective_id=0, has_side_effects=True),
    )(walker_m, vertex_times, vertex_labels, freq_index, q_index)


def solution(mesh):
    return jax.shard_map(
        local,
        mesh=mesh,
        in_specs=(
            P("walk", "blk", None, None),
            P("walk", "blk", None),
            P("walk", "blk", None),
            P(),
            P("blk"),
        ),
        out_specs=P("blk", None, "walk", None),
        check_vma=False,
    )
```

profile of v0, /device:TPU:0, one launch (start us, length us, event | category | flops | bytes accessed | tf_op | source)
XLA Modules:
  0.0 27.1 jit_solution(15274911547933692979)
XLA Ops:
  0.7 25.3 %shard_map.55 = f32[1,2,216,864]{3,2,1,0:T(8,128)S(1)} custom-call(bf16[1,1,128,128]{3,2,1,0:T(8,128)(2,1)} %m_in.1, s32[1,1,128]{2,1,0:T(1,128)} %t_in.1, s32[1,1,128]{2,1,0:T(1,128)} %l_in.1, s32[24]{0:T(128)} %freq_ref.1, s32[1]{0:T(128)S(6)} %copy.8.q_ref), custom_call_target="tpu_custom_call" | custom-call | tf_op jit(solution)/shard_map/pallas_call | solution.py:233
  26.0 1.1 %copy.7 = f32[1,2,216,864]{3,2,1,0:T(8,128)} copy(f32[1,2,216,864]{3,2,1,0:T(8,128)S(1)} %shard_map.55) | data formatting | bytes 2985984
where the time goes:
time: 27.3 us; the launch traced here: 27.1 us
  Pallas kernels  25.3 us (93%)
  local copies, waits for them, and re-layouts  1.14 us (4%)
  between operations  0.66 us (2%)
    pallas_call x1, Pallas kernels, local(): pl.pallas_call(functools.partial(kernel, groups, owners), out_shape=pltpu...  25.3 us
    unnamed x1, local copies, waits for them, and re-layouts  1.14 us

commit v1 on v0

--- a/solution.py
+++ b/solution.py
@@ -46,7 +46,7 @@
 def kernel(
     groups, owners, m_in, t_in, l_in, freq_ref, q_ref, out_ref,
     m_ref, t_ref, l_ref, send_sem, recv_sem,
-    odd, turn_c, turn_s, both, table, moved, left_a, left_b, left_c, right_b,
+    odd, plain, turned_m, table, lifted, left_s, left_f,
 ):
     order = visits(groups)
     walkers = len(order)
@@ -90,7 +90,7 @@
     m_ref[0] = m_in[0, 0]
     t_ref[0] = t_in[0]
     l_ref[0] = l_in[0]
-    both[...] = jnp.zeros_like(both)
+    plain[...] = jnp.zeros_like(plain)
     out_ref[...] = jnp.zeros_like(out_ref)
     pl.semaphore_wait(barrier, len(peers))
     for z, d in [o for o in order if o[0] and not o[1]] + [o for o in order if o[1] and not o[0]]:
@@ -107,10 +107,13 @@
 
     nf = freq_ref.shape[0]
     v = m_ref.shape[-1]
-    nk = SIDE * SIDE
-    own_k = out_ref.shape[2] // nf
+    own = out_ref.shape[2]
     cols = out_ref.shape[3]
-    first_k = w * own_k
+    window = lifted.shape[0]
+    first = w * own
+    spare = lax.rem(first, 16)
+    start = pl.multiple_of(first - spare, 16)
+    spare = pl.multiple_of(spare, 8)
 
     row = lax.broadcasted_iota(jnp.int32, (nf, v), 0)
     freq = jnp.zeros((nf, v), jnp.int32)
@@ -122,6 +125,82 @@
     qy = q - SIDE * qx
 
     scale = 1.0 / (v * v * walkers)
+    half = SIDE // 2
+    low, high = slice(0, v), slice(v, 2 * v)
+    contract = (((1,), (1,)), ((), ()))
+
+    def sites(slot):
+        labels = l_ref[slot]
+        sx = (labels * 43) >> 8
+        return sx, labels - SIDE * sx
+
+    def build_table(slot):
+        sx, sy = sites(slot)
+        units = (odd[...] * t_ref[slot]) & 2047
+        cx, ox = sixth_turn(sx)
+        cy, oy = sixth_turn(sy)
+        flip_x = (1 - 2 * (sx & 1)).astype(jnp.float32).astype(jnp.bfloat16)
+        flip_y = (1 - 2 * (sy & 1)).astype(jnp.float32)
+        c, s = sine(units + 512), sine(units)
+        for kx in range(half):
+            line = [(c, s)]
+            for ky in range(1, half):
+                c1, s1 = line[-1]
+                line.append((c1 * cy + s1 * oy, s1 * cy - c1 * oy))
+            line += [(c1 * flip_y, s1 * flip_y) for c1, s1 in line]
+            for pair in range(half):
+                rows = slice(nf * (SIDE * kx + 2 * pair), nf * (SIDE * kx + 2 * pair + 2))
+                far = slice(rows.start + nf * SIDE * half, rows.stop + nf * SIDE * half)
+                for side, lanes in enumerate((low, high)):
+                    both = jnp.concatenate(
+                        [line[2 * pair][side], line[2 * pair + 1][side]], axis=0
+                    ).astype(jnp.bfloat16)
+                    table[rows, lanes] = both
+                    table[far, lanes] = both * flip_x
+            c, s = c * cx + s * ox, s * cx - c * ox
+
+    def place_m(slot):
+        matrix = m_ref[slot]
+        plain[low, low] = matrix
+        plain[high, high] = matrix
+        sx, sy = sites(slot)
+        cu, su = sixth_turn(qx * sx + qy * sy)
+        cu = jnp.broadcast_to(cu, (v, v))
+        su = jnp.broadcast_to(su, (v, v))
+        ct, st = cu.T, su.T
+        wide = matrix.astype(jnp.float32) * scale
+        re = (wide * (ct * cu + st * su)).astype(jnp.bfloat16)
+        im = (wide * (ct * su - st * cu)).astype(jnp.bfloat16)
+        turned_m[low, low] = re
+        turned_m[high, high] = re
+        turned_m[low, high] = im
+        turned_m[high, low] = -im
+
+    def lift():
+        mine = table[pl.ds(start, window), :]
+        lifted[:, 0 : 2 * v] = jnp.dot(mine, turned_m[...], preferred_element_type=jnp.float32)
+        lifted[:, 2 * v : 4 * v] = lax.dot_general(
+            mine, plain[...], contract, preferred_element_type=jnp.float32
+        )
+        for ref, base in ((left_s, 0), (left_f, 2 * v)):
+            re = lifted[pl.ds(spare, own), base : base + v]
+            im = lifted[pl.ds(spare, own), base + v : base + 2 * v]
+            ref[:, low] = jnp.concatenate([re, im], axis=0).astype(jnp.bfloat16)
+            ref[:, high] = jnp.concatenate([im, -re], axis=0).astype(jnp.bfloat16)
+
+    def gather_terms():
+        for begin in range(0, cols, 256):
+            end = min(begin + 256, cols)
+            shifted = lax.dot_general(
+                left_s[...], table[begin:end], contract, preferred_element_type=jnp.float32
+            )
+            flipped = lax.dot_general(
+                left_f[...], table[begin:end], contract, preferred_element_type=jnp.float32
+            )
+            sr, si = shifted[:own], shifted[own:]
+            fr, fi = flipped[:own], flipped[own:]
+            out_ref[0, 0, :, begin:end] += sr * fr + si * fi
+            out_ref[0, 1, :, begin:end] += si * fr - sr * fi
 
     def step(visit, carry):
         swap = (lax.rem(b, 2) == 1) & ((visit == 1) | (visit == 2))
@@ -138,79 +217,10 @@
         def _():
             arrived(i)
 
-        matrix = m_ref[i]
-        both[0:v, 0:v] = matrix
-        both[v : 2 * v, v : 2 * v] = matrix
-        times = t_ref[i]
-        labels = l_ref[i]
-        sx = (labels * 43) >> 8
-        sy = labels - SIDE * sx
-        k = lax.broadcasted_iota(jnp.int32, turn_c.shape, 0)
-        kx = (k * 43) >> 8
-        ky = k - SIDE * kx
-        cosines, sines = sixth_turn(kx * sx + ky * sy)
-        turn_c[...] = cosines
-        turn_s[...] = sines
-        cq, sq = sixth_turn(qx * sx + qy * sy)
-
-        units = (odd[...] * times) & 2047
-        ca = sine(units + 512)
-        sa = sine(units)
-        ca_q = ca * cq + sa * sq
-        sa_q = sa * cq - ca * sq
-
-        def turned(c, s, k):
-            cb = turn_c[pl.ds(k, 1)]
-            sb = turn_s[pl.ds(k, 1)]
-            return c * cb + s * sb, s * cb - c * sb
-
-        def put(ref, place, first, second, lanes):
-            rows = slice(2 * nf * place, 2 * nf * (place + 1))
-            ref[rows, lanes] = jnp.concatenate([first, second], axis=0).astype(jnp.bfloat16)
-
-        low, high = slice(0, v), slice(v, 2 * v)
-        for pair in range(nk // 2):
-            c0, s0 = turned(ca, sa, 2 * pair)
-            c1, s1 = turned(ca, sa, 2 * pair + 1)
-            put(table, pair, c0, c1, low)
-            put(table, pair, s0, s1, high)
-            c0, s0 = turned(ca_q, sa_q, 2 * pair)
-            c1, s1 = turned(ca_q, sa_q, 2 * pair + 1)
-            put(moved, pair, c0, c1, low)
-            put(moved, pair, s0, s1, high)
-        for j in range(own_k):
-            c, s = turned(ca, sa, first_k + j)
-            put(left_b, j, c, -s, low)
-            put(left_b, j, s, c, high)
-            c, s = turned(ca_q, sa_q, first_k + j)
-            put(left_c, j, c, s, low)
-            put(left_c, j, s, -c, high)
-
-        right_b[...] = jnp.dot(
-            table[...], both[...], preferred_element_type=jnp.float32
-        ).astype(jnp.bfloat16)
-        product = jnp.dot(left_c[...], both[...], preferred_element_type=jnp.float32)
-        left_a[...] = (product.astype(jnp.bfloat16).astype(jnp.float32) * scale).astype(jnp.bfloat16)
-
-        contract = (((1,), (1,)), ((), ()))
-        for start in range(0, cols, 256):
-            stop = min(start + 256, cols)
-            shifted = lax.dot_general(
-                left_a[...], moved[start:stop], contract, preferred_element_type=jnp.float32
-            )
-            flipped = lax.dot_general(
-                left_b[...], right_b[start:stop], contract, preferred_element_type=jnp.float32
-            )
-            for j in range(own_k):
-                re = slice(2 * nf * j, 2 * nf * j + nf)
-                im = slice(2 * nf * j + nf, 2 * nf * (j + 1))
-                rows = slice(nf * j, nf * (j + 1))
-                out_ref[0, 0, rows, start:stop] += (
-                    shifted[re] * flipped[re] - shifted[im] * flipped[im]
-                )
-                out_ref[0, 1, rows, start:stop] += (
-                    shifted[re] * flipped[im] + shifted[im] * flipped[re]
-                )
+        build_table(i)
+        place_m(i)
+        lift()
+        gather_terms()
         return carry
 
     lax.fori_loop(0, walkers, step, 0)
@@ -227,6 +237,8 @@
     k = SIDE * SIDE * nf
     own = k // groups
     walkers = groups * len(OFFSETS)
+    window = own if own % 16 == 0 else (own + 23) // 16 * 16
+    held = max(k, max(own * w // 16 * 16 + window for w in range(groups)))
     vmem = pl.BlockSpec(memory_space=pltpu.VMEM)
     smem = pl.BlockSpec(memory_space=pltpu.SMEM)
     bf16 = jnp.bfloat16
@@ -242,15 +254,12 @@
             pltpu.SemaphoreType.DMA((3, walkers)),
             pltpu.SemaphoreType.DMA((3, walkers)),
             pltpu.VMEM((nf, v), jnp.int32),
-            pltpu.VMEM((40, v), jnp.float32),
-            pltpu.VMEM((40, v), jnp.float32),
             pltpu.VMEM((2 * v, 2 * v), bf16),
-            pltpu.VMEM((k, 2 * v), bf16),
-            pltpu.VMEM((k, 2 * v), bf16),
+            pltpu.VMEM((2 * v, 2 * v), bf16),
+            pltpu.VMEM((held, 2 * v), bf16),
+            pltpu.VMEM((window, 4 * v), jnp.float32),
             pltpu.VMEM((2 * own, 2 * v), bf16),
             pltpu.VMEM((2 * own, 2 * v), bf16),
-            pltpu.VMEM((2 * own, 2 * v), bf16),
-            pltpu.VMEM((k, 2 * v), bf16),
         ],
         compiler_params=pltpu.CompilerParams(collective_id=0, has_side_effects=True),
     )(walker_m, vertex_times, vertex_labels, freq_index, q_index)

time: 27.3 us -> 29.1 us (1.066)
  Pallas kernels: 25.3 us -> 27.1 us
    pallas_call x1, Pallas kernels: 25.3 us -> 27.1 us  [local(): pl.pallas_call(functools.partial(kernel, groups, owners), out_shape=pltpu...]
where the time goes in v1:
time: 29.1 us; the launch traced here: 28.9 us
  Pallas kernels  27.1 us (93%)
  local copies, waits for them, and re-layouts  1.14 us (4%)
  between operations  0.66 us (2%)
    pallas_call x1, Pallas kernels, local(): pl.pallas_call(functools.partial(kernel, groups, owners), out_shape=pltpu...  27.1 us
    unnamed x1, local copies, waits for them, and re-layouts  1.14 us

profile of v1, /device:TPU:0, one launch (start us, length us, event | category | flops | bytes accessed | tf_op | source)
XLA Modules:
  0.0 28.9 jit_solution(15521128319353356840)
XLA Ops:
  0.7 27.1 %shard_map.55 = f32[1,2,216,864]{3,2,1,0:T(8,128)S(1)} custom-call(bf16[1,1,128,128]{3,2,1,0:T(8,128)(2,1)} %m_in.1, s32[1,1,128]{2,1,0:T(1,128)} %t_in.1, s32[1,1,128]{2,1,0:T(1,128)} %l_in.1, s32[24]{0:T(128)} %freq_ref.1, s32[1]{0:T(128)S(6)} %copy.8.q_ref), custom_call_target="tpu_custom_call" | custom-call | tf_op jit(solution)/shard_map/pallas_call | solution.py:245
  27.8 1.1 %copy.7 = f32[1,2,216,864]{3,2,1,0:T(8,128)} copy(f32[1,2,216,864]{3,2,1,0:T(8,128)S(1)} %shard_map.55) | data formatting | bytes 2985984

commit v2 on v1

--- a/solution.py
+++ b/solution.py
@@ -46,7 +46,7 @@
 def kernel(
     groups, owners, m_in, t_in, l_in, freq_ref, q_ref, out_ref,
     m_ref, t_ref, l_ref, send_sem, recv_sem,
-    odd, plain, turned_m, table, lifted, left_s, left_f,
+    odd, plain, turned_m, table, left_s, left_f,
 ):
     order = visits(groups)
     walkers = len(order)
@@ -109,11 +109,10 @@
     v = m_ref.shape[-1]
     own = out_ref.shape[2]
     cols = out_ref.shape[3]
-    window = lifted.shape[0]
+    window = own if own % 16 == 0 else (own + 23) // 16 * 16
     first = w * own
     spare = lax.rem(first, 16)
     start = pl.multiple_of(first - spare, 16)
-    spare = pl.multiple_of(spare, 8)
 
     row = lax.broadcasted_iota(jnp.int32, (nf, v), 0)
     freq = jnp.zeros((nf, v), jnp.int32)
@@ -178,15 +177,18 @@
 
     def lift():
         mine = table[pl.ds(start, window), :]
-        lifted[:, 0 : 2 * v] = jnp.dot(mine, turned_m[...], preferred_element_type=jnp.float32)
-        lifted[:, 2 * v : 4 * v] = lax.dot_general(
-            mine, plain[...], contract, preferred_element_type=jnp.float32
-        )
-        for ref, base in ((left_s, 0), (left_f, 2 * v)):
-            re = lifted[pl.ds(spare, own), base : base + v]
-            im = lifted[pl.ds(spare, own), base + v : base + 2 * v]
-            ref[:, low] = jnp.concatenate([re, im], axis=0).astype(jnp.bfloat16)
-            ref[:, high] = jnp.concatenate([im, -re], axis=0).astype(jnp.bfloat16)
+        for ref, wide in (
+            (left_s, jnp.dot(mine, turned_m[...], preferred_element_type=jnp.float32)),
+            (left_f, lax.dot_general(mine, plain[...], contract, preferred_element_type=jnp.float32)),
+        ):
+            if window > own:
+                wide = jnp.where(spare > 0, wide[8 : 8 + own], wide[:own])
+            for tile in range(own // 8):
+                part = wide[8 * tile : 8 * tile + 8]
+                re, im = part[:, low], part[:, high]
+                rows = slice(16 * tile, 16 * tile + 16)
+                ref[rows, low] = jnp.concatenate([re, im], axis=0).astype(jnp.bfloat16)
+                ref[rows, high] = jnp.concatenate([im, -re], axis=0).astype(jnp.bfloat16)
 
     def gather_terms():
         for begin in range(0, cols, 256):
@@ -197,10 +199,12 @@
             flipped = lax.dot_general(
                 left_f[...], table[begin:end], contract, preferred_element_type=jnp.float32
             )
-            sr, si = shifted[:own], shifted[own:]
-            fr, fi = flipped[:own], flipped[own:]
-            out_ref[0, 0, :, begin:end] += sr * fr + si * fi
-            out_ref[0, 1, :, begin:end] += si * fr - sr * fi
+            for tile in range(own // 8):
+                re, im = slice(16 * tile, 16 * tile + 8), slice(16 * tile + 8, 16 * tile + 16)
+                rows = slice(8 * tile, 8 * tile + 8)
+                sr, si, fr, fi = shifted[re], shifted[im], flipped[re], flipped[im]
+                out_ref[0, 0, rows, begin:end] += sr * fr + si * fi
+                out_ref[0, 1, rows, begin:end] += si * fr - sr * fi
 
     def step(visit, carry):
         swap = (lax.rem(b, 2) == 1) & ((visit == 1) | (visit == 2))
@@ -257,7 +261,6 @@
             pltpu.VMEM((2 * v, 2 * v), bf16),
             pltpu.VMEM((2 * v, 2 * v), bf16),
             pltpu.VMEM((held, 2 * v), bf16),
-            pltpu.VMEM((window, 4 * v), jnp.float32),
             pltpu.VMEM((2 * own, 2 * v), bf16),
             pltpu.VMEM((2 * own, 2 * v), bf16),
         ],

time: 29.1 us -> 25.9 us (0.89)
  Pallas kernels: 27.1 us -> 23.9 us
    pallas_call x1, Pallas kernels: 27.1 us -> 23.9 us  [local(): pl.pallas_call(functools.partial(kernel, groups, owners), out_shape=pltpu...]
where the time goes in v2:
time: 25.9 us; the launch traced here: 25.7 us
  Pallas kernels  23.9 us (92%)
  local copies, waits for them, and re-layouts  1.14 us (4%)
  between operations  0.66 us (3%)
    pallas_call x1, Pallas kernels, local(): pl.pallas_call(functools.partial(kernel, groups, owners), out_shape=pltpu...  23.9 us
    unnamed x1, local copies, waits for them, and re-layouts  1.14 us

profile of v2, /device:TPU:0, one launch (start us, length us, event | category | flops | bytes accessed | tf_op | source)
XLA Modules:
  0.0 25.7 jit_solution(13175617916307504770)
XLA Ops:
  0.7 23.9 %shard_map.55 = f32[1,2,216,864]{3,2,1,0:T(8,128)S(1)} custom-call(bf16[1,1,128,128]{3,2,1,0:T(8,128)(2,1)} %m_in.1, s32[1,1,128]{2,1,0:T(1,128)} %t_in.1, s32[1,1,128]{2,1,0:T(1,128)} %l_in.1, s32[24]{0:T(128)} %freq_ref.1, s32[1]{0:T(128)S(6)} %copy.8.q_ref), custom_call_target="tpu_custom_call" | custom-call | tf_op jit(solution)/shard_map/pallas_call | solution.py:249
  24.6 1.1 %copy.7 = f32[1,2,216,864]{3,2,1,0:T(8,128)} copy(f32[1,2,216,864]{3,2,1,0:T(8,128)S(1)} %shard_map.55) | data formatting | bytes 2985984

commit v3 on v2

v3 whole, which is shorter than its diff:
```python
import functools
import math

import jax
import jax.numpy as jnp
from jax import lax
from jax.experimental import pallas as pl
from jax.experimental.pallas import tpu as pltpu
from jax.sharding import PartitionSpec as P

SIDE = 6
TGRID = 1024
OFFSETS = (0, 1, -1, 2)


def sine(units):
    wrapped = ((units + 1024) & 2047) - 1024
    folded = jnp.where(wrapped > 512, 1024 - wrapped, wrapped)
    folded = jnp.where(wrapped < -512, -1024 - wrapped, folded)
    x = folded.astype(jnp.float32) * (math.pi / 1024.0)
    y = x * x
    total = jnp.full_like(y, 1.0 / math.factorial(13))
    for order in (11, 9, 7, 5, 3, 1):
        sign = -1.0 if (order // 2) % 2 else 1.0
        total = total * y + sign / math.factorial(order)
    return total * x


def sixth_turn(m):
    r = m - 6 * ((m * 10923) >> 16)
    half = jnp.where((r == 1) | (r == 5), 0.5, -0.5)
    cosine = jnp.where(r == 0, 1.0, jnp.where(r == 3, -1.0, half))
    root = math.sqrt(3.0) / 2.0
    side = jnp.where(r < 3, root, -root)
    return cosine.astype(jnp.float32), jnp.where((r == 0) | (r == 3), 0.0, side).astype(jnp.float32)


def visits(groups):
    around = sorted(range(1, groups), key=lambda z: min(z, groups - z))
    near = [(0, d) for d in range(len(OFFSETS))]
    far = [(z, 0) for z in around]
    return near + far + [(z, d) for z in around for d in range(1, len(OFFSETS))]


def kernel(
    groups, owners, m_in, t_in, l_in, freq_ref, q_ref, out_ref,
    pack_ref, send_sem, recv_sem, odd, *stages,
):
    order = visits(groups)
    walkers = len(order)
    w = lax.axis_index("walk")
    b = lax.axis_index("blk")
    v = m_in.shape[-1]
    nf = freq_ref.shape[0]
    own = out_ref.shape[2]
    cols = out_ref.shape[3]
    even, odds = stages[: len(stages) // 2], stages[len(stages) // 2 :]

    def to_walk(z):
        return {"walk": lax.rem(w + groups - z, groups)}

    def to_blk(d):
        return {"blk": lax.rem(b + owners - OFFSETS[d], owners)}

    def copy(source, slot, device):
        return pltpu.make_async_remote_copy(
            src_ref=pack_ref.at[source],
            dst_ref=pack_ref.at[slot],
            send_sem=send_sem.at[slot],
            recv_sem=recv_sem.at[slot],
            device_id=device,
            device_id_type=pl.DeviceIdType.MESH,
        )

    def arrived(slot):
        copy(0, slot, to_walk(1)).wait_recv()

    def forward(slot):
        z = order[slot][0]
        for d in range(1, len(OFFSETS)):
            copy(slot, order.index((z, d)), to_blk(d)).start()

    barrier = pltpu.get_barrier_semaphore()
    peers = [{"walk": lax.rem(w + z, groups)} for z in range(1, groups)]
    reach = sorted({d % owners for d in OFFSETS + tuple(-d for d in OFFSETS)} - {0})
    peers += [{"blk": lax.rem(b + d, owners)} for d in reach]
    for peer in peers:
        pl.semaphore_signal(barrier, inc=1, device_id=peer, device_id_type=pl.DeviceIdType.MESH)

    pack_ref[0, 0:v] = m_in[0, 0]
    times = t_in[0]
    line = lax.broadcasted_iota(jnp.int32, (16, v), 0)
    notes = jnp.where(line == 0, times >> 5, jnp.where(line == 1, times & 31, l_in[0]))
    pack_ref[0, v : v + 16] = notes.astype(jnp.float32).astype(jnp.bfloat16)

    window = own if own % 16 == 0 else (own + 23) // 16 * 16
    first = w * own
    spare = lax.rem(first, 16)
    start = pl.multiple_of(first - spare, 16)

    row = lax.broadcasted_iota(jnp.int32, (nf, v), 0)
    freq = jnp.zeros((nf, v), jnp.int32)
    for f in range(nf):
        freq = jnp.where(row == f, 2 * freq_ref[f] + 1, freq)
    odd[...] = freq
    q = q_ref[0]
    qx = (q * 43) >> 8
    qy = q - SIDE * qx

    scale = 1.0 / (v * v * walkers)
    half = SIDE // 2
    low, high = slice(0, v), slice(v, 2 * v)
    contract = (((1,), (1,)), ((), ()))

    for plain, *_ in (even, odds):
        plain[...] = jnp.zeros_like(plain)

    def prepare(slot, stage):
        plain, turned_m, table, left_s, left_f = stage
        notes = pack_ref[slot, v : v + 16].astype(jnp.float32).astype(jnp.int32)
        times = (notes[0:1] << 5) + notes[1:2]
        labels = notes[2:3]
        sx = (labels * 43) >> 8
        sy = labels - SIDE * sx

        matrix = pack_ref[slot, 0:v]
        plain[low, low] = matrix
        plain[high, high] = matrix
        cu, su = sixth_turn(qx * sx + qy * sy)
        cu = jnp.broadcast_to(cu, (v, v))
        su = jnp.broadcast_to(su, (v, v))
        ct, st = cu.T, su.T
        wide = matrix.astype(jnp.float32) * scale
        re = (wide * (ct * cu + st * su)).astype(jnp.bfloat16)
        im = (wide * (ct * su - st * cu)).astype(jnp.bfloat16)
        turned_m[low, low] = re
        turned_m[high, high] = re
        turned_m[low, high] = im
        turned_m[high, low] = -im

        units = (odd[...] * times) & 2047
        cx, ox = sixth_turn(sx)
        cy, oy = sixth_turn(sy)
        flip_x = (1 - 2 * (sx & 1)).astype(jnp.float32).astype(jnp.bfloat16)
        flip_y = (1 - 2 * (sy & 1)).astype(jnp.float32)
        c, s = sine(units + 512), sine(units)
        for kx in range(half):
            line = [(c, s)]
            for ky in range(1, half):
                c1, s1 = line[-1]
                line.append((c1 * cy + s1 * oy, s1 * cy - c1 * oy))
            line += [(c1 * flip_y, s1 * flip_y) for c1, s1 in line]
            for pair in range(half):
                rows = slice(nf * (SIDE * kx + 2 * pair), nf * (SIDE * kx + 2 * pair + 2))
                far = slice(rows.start + nf * SIDE * half, rows.stop + nf * SIDE * half)
                for side, lanes in enumerate((low, high)):
                    both = jnp.concatenate(
                        [line[2 * pair][side], line[2 * pair + 1][side]], axis=0
                    ).astype(jnp.bfloat16)
                    table[rows, lanes] = both
                    table[far, lanes] = both * flip_x
            c, s = c * cx + s * ox, s * cx - c * ox

        mine = table[pl.ds(start, window), :]
        for ref, wide in (
            (left_s, jnp.dot(mine, turned_m[...], preferred_element_type=jnp.float32)),
            (left_f, lax.dot_general(mine, plain[...], contract, preferred_element_type=jnp.float32)),
        ):
            if window > own:
                wide = jnp.where(spare > 0, wide[8 : 8 + own], wide[:own])
            for tile in range(own // 8):
                part = wide[8 * tile : 8 * tile + 8]
                re, im = part[:, low], part[:, high]
                rows = slice(16 * tile, 16 * tile + 16)
                ref[rows, low] = jnp.concatenate([re, im], axis=0).astype(jnp.bfloat16)
                ref[rows, high] = jnp.concatenate([im, -re], axis=0).astype(jnp.bfloat16)

    def gather_terms(stage, begun=True):
        plain, turned_m, table, left_s, left_f = stage
        for begin in range(0, cols, 256):
            end = min(begin + 256, cols)
            shifted = lax.dot_general(
                left_s[...], table[begin:end], contract, preferred_element_type=jnp.float32
            )
            flipped = lax.dot_general(
                left_f[...], table[begin:end], contract, preferred_element_type=jnp.float32
            )
            for tile in range(own // 8):
                re, im = slice(16 * tile, 16 * tile + 8), slice(16 * tile + 8, 16 * tile + 16)
                rows = slice(8 * tile, 8 * tile + 8)
                sr, si, fr, fi = shifted[re], shifted[im], flipped[re], flipped[im]
                term_re, term_im = sr * fr + si * fi, si * fr - sr * fi
                if begun:
                    out_ref[0, 0, rows, begin:end] += term_re
                    out_ref[0, 1, rows, begin:end] += term_im
                else:
                    out_ref[0, 0, rows, begin:end] = term_re
                    out_ref[0, 1, rows, begin:end] = term_im

    prepare(0, even)
    pl.semaphore_wait(barrier, len(peers))
    for z, d in [o for o in order if o[0] and not o[1]] + [o for o in order if o[1] and not o[0]]:
        copy(0, order.index((z, d)), to_walk(z) if z else to_blk(d)).start()
    gather_terms(even, begun=False)

    turned = lax.rem(b, 2)
    near = len(OFFSETS)
    arrived(1 + turned)
    prepare(1 + turned, odds)

    def step(turn, carry):
        for later, (ready, coming) in enumerate(((odds, even), (even, odds))):
            visit = 2 * turn + 2 + later
            slot = jnp.where(turn == 0, 2 - turned, visit) if later == 0 else visit
            arrived(slot)
            for far in range(near, near + groups - 1):
                if far % 2 == later:
                    @pl.when(turn == (far - 2) // 2)
                    def _(far=far):
                        forward(far)
            if later == 0:
                first_slot = slot
        prepare(first_slot, even)
        gather_terms(odds)
        prepare(visit, odds)
        gather_terms(even)
        return carry

    lax.fori_loop(0, walkers // 2 - 1, step, 0)
    gather_terms(odds)
    for slot in range(1, walkers):
        copy(0, slot, to_walk(1)).wait_send()


def local(walker_m, vertex_times, vertex_labels, freq_index, q_index):
    groups = lax.axis_size("walk")
    owners = lax.axis_size("blk")
    v = walker_m.shape[-1]
    nf = freq_index.shape[0]
    k = SIDE * SIDE * nf
    own = k // groups
    walkers = groups * len(OFFSETS)
    window = own if own % 16 == 0 else (own + 23) // 16 * 16
    held = max(k, max(own * w // 16 * 16 + window for w in range(groups)))
    vmem = pl.BlockSpec(memory_space=pltpu.VMEM)
    smem = pl.BlockSpec(memory_space=pltpu.SMEM)
    bf16 = jnp.bfloat16
    stage = [
        pltpu.VMEM((2 * v, 2 * v), bf16),
        pltpu.VMEM((2 * v, 2 * v), bf16),
        pltpu.VMEM((held, 2 * v), bf16),
        pltpu.VMEM((2 * own, 2 * v), bf16),
        pltpu.VMEM((2 * own, 2 * v), bf16),
    ]
    return pl.pallas_call(
        functools.partial(kernel, groups, owners),
        out_shape=pltpu.VMEM((1, 2, own, k), jnp.float32),
        in_specs=[vmem, vmem, vmem, smem, smem],
        out_specs=vmem,
        scratch_shapes=[
            pltpu.VMEM((walkers, v + 16, v), bf16),
            pltpu.SemaphoreType.DMA((walkers,)),
            pltpu.SemaphoreType.DMA((walkers,)),
            pltpu.VMEM((nf, v), jnp.int32),
            *stage,
            *stage,
        ],
        compiler_params=pltpu.CompilerParams(collective_id=0, has_side_effects=True),
    )(walker_m, vertex_times, vertex_labels, freq_index, q_index)


def solution(mesh):
    return jax.shard_map(
        local,
        mesh=mesh,
        in_specs=(
            P("walk", "blk", None, None),
            P("walk", "blk", None),
            P("walk", "blk", None),
            P(),
            P("blk"),
        ),
        out_specs=P("blk", None, "walk", None),
        check_vma=False,
    )
```

time: 25.9 us -> 25.3 us (0.977)
  the two profiles are of different devices: /device:TPU:0 before, /device:TPU:1 now
where the time goes in v3:
time: 25.3 us; the launch traced here: 25.1 us
  Pallas kernels  23.3 us (92%)
  local copies, waits for them, and re-layouts  1.14 us (5%)
  between operations  0.66 us (3%)
    pallas_call x1, Pallas kernels, local(): pl.pallas_call(functools.partial(kernel, groups, owners), out_shape=pltpu...  23.3 us
    unnamed x1, local copies, waits for them, and re-layouts  1.14 us

profile of v3, /device:TPU:1, one launch (start us, length us, event | category | flops | bytes accessed | tf_op | source)
XLA Modules:
  0.0 25.1 jit_solution(12068854927951369399)
XLA Ops:
  0.7 23.3 %shard_map.55 = f32[1,2,216,864]{3,2,1,0:T(8,128)S(1)} custom-call(bf16[1,1,128,128]{3,2,1,0:T(8,128)(2,1)} %m_in.1, s32[1,1,128]{2,1,0:T(1,128)} %t_in.1, s32[1,1,128]{2,1,0:T(1,128)} %l_in.1, s32[24]{0:T(128)} %freq_ref.1, s32[1]{0:T(128)S(6)} %copy.8.q_ref), custom_call_target="tpu_custom_call" | custom-call | tf_op jit(solution)/shard_map/pallas_call | solution.py:255
  24.0 1.1 %copy.7 = f32[1,2,216,864]{3,2,1,0:T(8,128)} copy(f32[1,2,216,864]{3,2,1,0:T(8,128)S(1)} %shard_map.55) | data formatting | bytes 2985984

commit v4 on v3

--- a/solution.py
+++ b/solution.py
@@ -36,10 +36,21 @@
 
 
 def visits(groups):
-    around = sorted(range(1, groups), key=lambda z: min(z, groups - z))
-    near = [(0, d) for d in range(len(OFFSETS))]
-    far = [(z, 0) for z in around]
-    return near + far + [(z, d) for z in around for d in range(1, len(OFFSETS))]
+    rest = range(1, len(OFFSETS))
+    far = [(z, 0) for z in range(1, groups)]
+    start = [(0, 0), (0, 1), (0, 2)] + far[:1] + [(0, 3)] + far[1:]
+    return start + [(z, d) for z in range(1, groups) for d in rest]
+
+
+def across(w, z, groups):
+    if groups & (groups - 1):
+        return lax.rem(w + groups - z, groups)
+    bit, there = 1, w
+    while bit < groups:
+        if z & bit:
+            there = there + bit - 2 * bit * lax.rem(w // bit, 2)
+        bit *= 2
+    return there
 
 
 def kernel(
@@ -56,11 +67,9 @@
     cols = out_ref.shape[3]
     even, odds = stages[: len(stages) // 2], stages[len(stages) // 2 :]
 
-    def to_walk(z):
-        return {"walk": lax.rem(w + groups - z, groups)}
-
-    def to_blk(d):
-        return {"blk": lax.rem(b + owners - OFFSETS[d], owners)}
+    def place(z, d):
+        where = {"blk": lax.rem(b + owners - OFFSETS[d], owners)} if d else {}
+        return where | ({"walk": across(w, z, groups)} if z else {})
 
     def copy(source, slot, device):
         return pltpu.make_async_remote_copy(
@@ -73,17 +82,19 @@
         )
 
     def arrived(slot):
-        copy(0, slot, to_walk(1)).wait_recv()
+        copy(0, slot, place(1, 0)).wait_recv()
 
     def forward(slot):
         z = order[slot][0]
         for d in range(1, len(OFFSETS)):
-            copy(slot, order.index((z, d)), to_blk(d)).start()
+            copy(slot, order.index((z, d)), place(0, d)).start()
 
     barrier = pltpu.get_barrier_semaphore()
     peers = [{"walk": lax.rem(w + z, groups)} for z in range(1, groups)]
     reach = sorted({d % owners for d in OFFSETS + tuple(-d for d in OFFSETS)} - {0})
     peers += [{"blk": lax.rem(b + d, owners)} for d in reach]
+    beside = [across(w, 1, groups)] + ([lax.rem(w + 1, groups)] if groups & (groups - 1) else [])
+    peers += [{"blk": lax.rem(b + d, owners), "walk": z} for d in reach for z in beside]
     for peer in peers:
         pl.semaphore_signal(barrier, inc=1, device_id=peer, device_id_type=pl.DeviceIdType.MESH)
 
@@ -199,12 +210,12 @@
 
     prepare(0, even)
     pl.semaphore_wait(barrier, len(peers))
-    for z, d in [o for o in order if o[0] and not o[1]] + [o for o in order if o[1] and not o[0]]:
-        copy(0, order.index((z, d)), to_walk(z) if z else to_blk(d)).start()
+    for slot, (z, d) in enumerate(order):
+        if slot and (not z or not d or z == 1):
+            copy(0, slot, place(z, d)).start()
     gather_terms(even, begun=False)
 
     turned = lax.rem(b, 2)
-    near = len(OFFSETS)
     arrived(1 + turned)
     prepare(1 + turned, odds)
 
@@ -213,11 +224,11 @@
             visit = 2 * turn + 2 + later
             slot = jnp.where(turn == 0, 2 - turned, visit) if later == 0 else visit
             arrived(slot)
-            for far in range(near, near + groups - 1):
-                if far % 2 == later:
-                    @pl.when(turn == (far - 2) // 2)
-                    def _(far=far):
-                        forward(far)
+            for relay, (z, d) in enumerate(order):
+                if z > 1 and not d and relay % 2 == later:
+                    @pl.when(turn == (relay - 2) // 2)
+                    def _(relay=relay):
+                        forward(relay)
             if later == 0:
                 first_slot = slot
         prepare(first_slot, even)
@@ -229,7 +240,7 @@
     lax.fori_loop(0, walkers // 2 - 1, step, 0)
     gather_terms(odds)
     for slot in range(1, walkers):
-        copy(0, slot, to_walk(1)).wait_send()
+        copy(0, slot, place(1, 0)).wait_send()
 
 
 def local(walker_m, vertex_times, vertex_labels, freq_index, q_index):

time: 25.3 us -> 23 us (0.909)
  the two profiles are of different devices: /device:TPU:1 before, /device:TPU:0 now
where the time goes in v4:
time: 23 us; the launch traced here: 22.8 us
  Pallas kernels  21 us (91%)
  local copies, waits for them, and re-layouts  1.14 us (5%)
  between operations  0.66 us (3%)
    pallas_call x1, Pallas kernels, local(): pl.pallas_call(functools.partial(kernel, groups, owners), out_shape=pltpu...  21 us
    unnamed x1, local copies, waits for them, and re-layouts  1.14 us

profile of v4, /device:TPU:0, one launch (start us, length us, event | category | flops | bytes accessed | tf_op | source)
XLA Modules:
  0.0 22.8 jit_solution(3060437399720046479)
XLA Ops:
  0.7 21.0 %shard_map.55 = f32[1,2,216,864]{3,2,1,0:T(8,128)S(1)} custom-call(bf16[1,1,128,128]{3,2,1,0:T(8,128)(2,1)} %m_in.1, s32[1,1,128]{2,1,0:T(1,128)} %t_in.1, s32[1,1,128]{2,1,0:T(1,128)} %l_in.1, s32[24]{0:T(128)} %freq_ref.1, s32[1]{0:T(128)S(6)} %copy.8.q_ref), custom_call_target="tpu_custom_call" | custom-call | tf_op jit(solution)/shard_map/pallas_call | solution.py:266
  21.7 1.1 %copy.7 = f32[1,2,216,864]{3,2,1,0:T(8,128)} copy(f32[1,2,216,864]{3,2,1,0:T(8,128)S(1)} %shard_map.55) | data formatting | bytes 2985984

commit v5 on v4

--- a/solution.py
+++ b/solution.py
@@ -11,6 +11,9 @@
 SIDE = 6
 TGRID = 1024
 OFFSETS = (0, 1, -1, 2)
+EVERY = 2
+SENDS = ((0, 1), (0, 2), (1, 0), (0, 3), (2, 0), (3, 0))
+PLAN = (0, 0, 0, 0)
 
 
 def sine(units):
@@ -36,10 +39,10 @@
 
 
 def visits(groups):
-    rest = range(1, len(OFFSETS))
-    far = [(z, 0) for z in range(1, groups)]
-    start = [(0, 0), (0, 1), (0, 2)] + far[:1] + [(0, 3)] + far[1:]
-    return start + [(z, d) for z in range(1, groups) for d in rest]
+    order = [(0, 0), (0, "p"), (0, "c"), (1, 0), (0, 3), (1, "p")]
+    order += [(z, 0) for z in range(2, groups)] + [(1, "c"), (1, 3)]
+    order += [(z, "p") for z in range(2, groups)]
+    return order + [(z, d) for z in range(2, groups) for d in ("c", 3)]
 
 
 def across(w, z, groups):
@@ -57,8 +60,8 @@
     groups, owners, m_in, t_in, l_in, freq_ref, q_ref, out_ref,
     pack_ref, send_sem, recv_sem, odd, *stages,
 ):
-    order = visits(groups)
-    walkers = len(order)
+    walkers = groups * len(OFFSETS)
+    order = [(z, d) for z in range(groups) for d in range(len(OFFSETS))]
     w = lax.axis_index("walk")
     b = lax.axis_index("blk")
     v = m_in.shape[-1]
@@ -84,17 +87,14 @@
     def arrived(slot):
         copy(0, slot, place(1, 0)).wait_recv()
 
-    def forward(slot):
-        z = order[slot][0]
+    def forward(z):
         for d in range(1, len(OFFSETS)):
-            copy(slot, order.index((z, d)), place(0, d)).start()
+            copy(order.index((z, 0)), order.index((z, d)), place(0, d)).start()
 
     barrier = pltpu.get_barrier_semaphore()
     peers = [{"walk": lax.rem(w + z, groups)} for z in range(1, groups)]
     reach = sorted({d % owners for d in OFFSETS + tuple(-d for d in OFFSETS)} - {0})
     peers += [{"blk": lax.rem(b + d, owners)} for d in reach]
-    beside = [across(w, 1, groups)] + ([lax.rem(w + 1, groups)] if groups & (groups - 1) else [])
-    peers += [{"blk": lax.rem(b + d, owners), "walk": z} for d in reach for z in beside]
     for peer in peers:
         pl.semaphore_signal(barrier, inc=1, device_id=peer, device_id_type=pl.DeviceIdType.MESH)
 
@@ -149,6 +149,7 @@
         turned_m[low, high] = im
         turned_m[high, low] = -im
 
+        yield
         units = (odd[...] * times) & 2047
         cx, ox = sixth_turn(sx)
         cy, oy = sixth_turn(sy)
@@ -171,6 +172,7 @@
                     table[rows, lanes] = both
                     table[far, lanes] = both * flip_x
             c, s = c * cx + s * ox, s * cx - c * ox
+            yield
 
         mine = table[pl.ds(start, window), :]
         for ref, wide in (
@@ -185,6 +187,7 @@
                 rows = slice(16 * tile, 16 * tile + 16)
                 ref[rows, low] = jnp.concatenate([re, im], axis=0).astype(jnp.bfloat16)
                 ref[rows, high] = jnp.concatenate([im, -re], axis=0).astype(jnp.bfloat16)
+            yield
 
     def gather_terms(stage, begun=True):
         plain, turned_m, table, left_s, left_f = stage
@@ -207,38 +210,45 @@
                 else:
                     out_ref[0, 0, rows, begin:end] = term_re
                     out_ref[0, 1, rows, begin:end] = term_im
-
-    prepare(0, even)
+            yield
+
+    def run(plan, *parts):
+        for part in plan:
+            next(parts[part], None)
+        for part in parts:
+            for _ in part:
+                pass
+
+    turned = lax.rem(b, 2)
+
+    def held(visit):
+        z, d = plan[visit]
+        d = {"p": 1 + turned, "c": 2 - turned}.get(d, d)
+        return z * len(OFFSETS) + d
+
+    def await_visits(*coming):
+        for visit in coming:
+            if visit < walkers:
+                arrived(held(visit))
+                z, d = plan[visit]
+                if z and not d:
+                    forward(z)
+
+    plan = visits(groups)
+    run((), prepare(0, even))
     pl.semaphore_wait(barrier, len(peers))
-    for slot, (z, d) in enumerate(order):
-        if slot and (not z or not d or z == 1):
-            copy(0, slot, place(z, d)).start()
-    gather_terms(even, begun=False)
-
-    turned = lax.rem(b, 2)
-    arrived(1 + turned)
-    prepare(1 + turned, odds)
-
-    def step(turn, carry):
-        for later, (ready, coming) in enumerate(((odds, even), (even, odds))):
-            visit = 2 * turn + 2 + later
-            slot = jnp.where(turn == 0, 2 - turned, visit) if later == 0 else visit
-            arrived(slot)
-            for relay, (z, d) in enumerate(order):
-                if z > 1 and not d and relay % 2 == later:
-                    @pl.when(turn == (relay - 2) // 2)
-                    def _(relay=relay):
-                        forward(relay)
-            if later == 0:
-                first_slot = slot
-        prepare(first_slot, even)
-        gather_terms(odds)
-        prepare(visit, odds)
-        gather_terms(even)
-        return carry
-
-    lax.fori_loop(0, walkers // 2 - 1, step, 0)
-    gather_terms(odds)
+    for z, d in SENDS:
+        if z < groups:
+            copy(0, order.index((z, d)), place(z, d)).start()
+    run((), gather_terms(even, begun=False))
+    await_visits(1)
+    run((), prepare(held(1), odds))
+    for visit in range(2, walkers, EVERY):
+        await_visits(*range(visit, min(visit + EVERY, walkers)))
+        for coming in range(visit, min(visit + EVERY, walkers)):
+            now, then = (odds, even) if coming % 2 == 0 else (even, odds)
+            run(PLAN, gather_terms(now), prepare(held(coming), then))
+    run((), gather_terms(odds))
     for slot in range(1, walkers):
         copy(0, slot, place(1, 0)).wait_send()
 

time: 23 us -> 22 us (0.957)
  Pallas kernels: 21 us -> 20 us
    pallas_call x1, Pallas kernels: 21 us -> 20 us  [local(): pl.pallas_call(functools.partial(kernel, groups, owners), out_shape=pltpu...]
where the time goes in v5:
time: 22 us; the launch traced here: 21.8 us
  Pallas kernels  20 us (91%)
  local copies, waits for them, and re-layouts  1.14 us (5%)
  between operations  0.66 us (3%)
    pallas_call x1, Pallas kernels, local(): pl.pallas_call(functools.partial(kernel, groups, owners), out_shape=pltpu...  20 us
    unnamed x1, local copies, waits for them, and re-layouts  1.14 us

profile of v5, /device:TPU:0, one launch (start us, length us, event | category | flops | bytes accessed | tf_op | source)
XLA Modules:
  0.0 21.8 jit_solution(14336122440298470019)
XLA Ops:
  0.7 20.0 %shard_map.55 = f32[1,2,216,864]{3,2,1,0:T(8,128)S(1)} custom-call(bf16[1,1,128,128]{3,2,1,0:T(8,128)(2,1)} %m_in.1, s32[1,1,128]{2,1,0:T(1,128)} %t_in.1, s32[1,1,128]{2,1,0:T(1,128)} %l_in.1, s32[24]{0:T(128)} %freq_ref.1, s32[1]{0:T(128)S(6)} %copy.8.q_ref), custom_call_target="tpu_custom_call" | custom-call | tf_op jit(solution)/shard_map/pallas_call | solution.py:276
  20.7 1.1 %copy.7 = f32[1,2,216,864]{3,2,1,0:T(8,128)} copy(f32[1,2,216,864]{3,2,1,0:T(8,128)S(1)} %shard_map.55) | data formatting | bytes 2985984

commit v6 on v5

--- a/solution.py
+++ b/solution.py
@@ -11,9 +11,6 @@
 SIDE = 6
 TGRID = 1024
 OFFSETS = (0, 1, -1, 2)
-EVERY = 2
-SENDS = ((0, 1), (0, 2), (1, 0), (0, 3), (2, 0), (3, 0))
-PLAN = (0, 0, 0, 0)
 
 
 def sine(units):
@@ -39,10 +36,27 @@
 
 
 def visits(groups):
-    order = [(0, 0), (0, "p"), (0, "c"), (1, 0), (0, 3), (1, "p")]
-    order += [(z, 0) for z in range(2, groups)] + [(1, "c"), (1, 3)]
-    order += [(z, "p") for z in range(2, groups)]
-    return order + [(z, d) for z in range(2, groups) for d in ("c", 3)]
+    order = [(0, 0), (0, "p"), (1, 0), (0, "c"), (1, "p")]
+    order += [(z, 0) for z in range(2, min(groups, 3))] + [(0, 3)]
+    order += [(z, 0) for z in range(3, groups)] + [(1, "c"), (1, 3)]
+    order += [(z, "p") for z in range(2, groups)] + [(z, "c") for z in range(2, groups)]
+    return order + [(z, 3) for z in range(2, groups)]
+
+
+def blocks(walkers):
+    out = [((1,), "T1 L1 G1"), ((2,), "T2 L2"), ((3,), "g2 g2 T3 L3 G2")]
+    out.append(((4, 5), "g3 g3 g3 T4 L4 G3 g4 g4 g4 T5 L5 G4"))
+    out.append(((6, 7, 8), "g5 g5 g5 T6 L6 G5 T7 g6 g6 L7 G6 T8"))
+    done, ready = 6, 9
+    while done < walkers - 1:
+        coming = tuple(range(ready, min(ready + 2, walkers)))
+        ops = []
+        for step in range(2 if ready + 2 <= walkers else walkers - 1 - done):
+            done += 1
+            ops += [f"g{done}"] * 1 + [f"L{done + 1}"] * (done + 1 < walkers) + [f"T{done + 2}"] * (done + 2 < walkers) + [f"G{done}"]
+        ready += len(coming)
+        out.append((coming, " ".join(ops)))
+    return out
 
 
 def across(w, z, groups):
@@ -58,7 +72,7 @@
 
 def kernel(
     groups, owners, m_in, t_in, l_in, freq_ref, q_ref, out_ref,
-    pack_ref, send_sem, recv_sem, odd, *stages,
+    pack_ref, send_sem, recv_sem, relay_sem, odd, *stages,
 ):
     walkers = groups * len(OFFSETS)
     order = [(z, d) for z in range(groups) for d in range(len(OFFSETS))]
@@ -68,17 +82,21 @@
     nf = freq_ref.shape[0]
     own = out_ref.shape[2]
     cols = out_ref.shape[3]
-    even, odds = stages[: len(stages) // 2], stages[len(stages) // 2 :]
+    tables = [stages[3 * i : 3 * i + 3] for i in range(3)]
+    lefts = [stages[9 + 2 * i : 11 + 2 * i] for i in range(2)]
 
     def place(z, d):
         where = {"blk": lax.rem(b + owners - OFFSETS[d], owners)} if d else {}
         return where | ({"walk": across(w, z, groups)} if z else {})
 
-    def copy(source, slot, device):
+    turned = lax.rem(b, 2)
+    beside = {"blk": b + 1 - 2 * turned}
+
+    def copy(source, slot, device, sent=None):
         return pltpu.make_async_remote_copy(
             src_ref=pack_ref.at[source],
             dst_ref=pack_ref.at[slot],
-            send_sem=send_sem.at[slot],
+            send_sem=send_sem.at[slot] if sent is None else relay_sem.at[sent],
             recv_sem=recv_sem.at[slot],
             device_id=device,
             device_id_type=pl.DeviceIdType.MESH,
@@ -87,9 +105,17 @@
     def arrived(slot):
         copy(0, slot, place(1, 0)).wait_recv()
 
-    def forward(z):
-        for d in range(1, len(OFFSETS)):
-            copy(order.index((z, 0)), order.index((z, d)), place(0, d)).start()
+    def relay(z):
+        return copy(order.index((z, 1)), order.index((z, 3)), beside, z)
+
+    def spread(z):
+        here = order.index((z, 0))
+        for d in (1, 2):
+            copy(here, order.index((z, d)), place(0, d)).start()
+
+        @pl.when(turned == 1)
+        def _():
+            copy(here, order.index((z, 3)), place(0, 3)).start()
 
     barrier = pltpu.get_barrier_semaphore()
     peers = [{"walk": lax.rem(w + z, groups)} for z in range(1, groups)]
@@ -100,9 +126,9 @@
 
     pack_ref[0, 0:v] = m_in[0, 0]
     times = t_in[0]
-    line = lax.broadcasted_iota(jnp.int32, (16, v), 0)
+    line = lax.broadcasted_iota(jnp.int32, (8, v), 0)
     notes = jnp.where(line == 0, times >> 5, jnp.where(line == 1, times & 31, l_in[0]))
-    pack_ref[0, v : v + 16] = notes.astype(jnp.float32).astype(jnp.bfloat16)
+    pack_ref[0, v : v + 8] = notes.astype(jnp.float32).astype(jnp.bfloat16)
 
     window = own if own % 16 == 0 else (own + 23) // 16 * 16
     first = w * own
@@ -123,12 +149,12 @@
     low, high = slice(0, v), slice(v, 2 * v)
     contract = (((1,), (1,)), ((), ()))
 
-    for plain, *_ in (even, odds):
+    for plain, _, _ in tables:
         plain[...] = jnp.zeros_like(plain)
-
-    def prepare(slot, stage):
-        plain, turned_m, table, left_s, left_f = stage
-        notes = pack_ref[slot, v : v + 16].astype(jnp.float32).astype(jnp.int32)
+    def tabulate(visit):
+        slot = held(visit)
+        plain, turned_m, table = tables[visit % len(tables)]
+        notes = pack_ref[slot, v : v + 8].astype(jnp.float32).astype(jnp.int32)
         times = (notes[0:1] << 5) + notes[1:2]
         labels = notes[2:3]
         sx = (labels * 43) >> 8
@@ -149,7 +175,6 @@
         turned_m[low, high] = im
         turned_m[high, low] = -im
 
-        yield
         units = (odd[...] * times) & 2047
         cx, ox = sixth_turn(sx)
         cy, oy = sixth_turn(sy)
@@ -172,8 +197,10 @@
                     table[rows, lanes] = both
                     table[far, lanes] = both * flip_x
             c, s = c * cx + s * ox, s * cx - c * ox
-            yield
-
+
+    def lift(visit):
+        plain, turned_m, table = tables[visit % len(tables)]
+        left_s, left_f = lefts[visit % len(lefts)]
         mine = table[pl.ds(start, window), :]
         for ref, wide in (
             (left_s, jnp.dot(mine, turned_m[...], preferred_element_type=jnp.float32)),
@@ -187,10 +214,18 @@
                 rows = slice(16 * tile, 16 * tile + 16)
                 ref[rows, low] = jnp.concatenate([re, im], axis=0).astype(jnp.bfloat16)
                 ref[rows, high] = jnp.concatenate([im, -re], axis=0).astype(jnp.bfloat16)
-            yield
-
-    def gather_terms(stage, begun=True):
-        plain, turned_m, table, left_s, left_f = stage
+
+    def gather_terms(visit):
+        table = tables[visit % len(tables)][2]
+        left_s, left_f = lefts[visit % len(lefts)]
+        begun = visit > 0
+
+        def add(ref, place, term):
+            if begun:
+                ref[place] += term
+            else:
+                ref[place] = term
+
         for begin in range(0, cols, 256):
             end = min(begin + 256, cols)
             shifted = lax.dot_general(
@@ -203,54 +238,62 @@
                 re, im = slice(16 * tile, 16 * tile + 8), slice(16 * tile + 8, 16 * tile + 16)
                 rows = slice(8 * tile, 8 * tile + 8)
                 sr, si, fr, fi = shifted[re], shifted[im], flipped[re], flipped[im]
-                term_re, term_im = sr * fr + si * fi, si * fr - sr * fi
-                if begun:
-                    out_ref[0, 0, rows, begin:end] += term_re
-                    out_ref[0, 1, rows, begin:end] += term_im
-                else:
-                    out_ref[0, 0, rows, begin:end] = term_re
-                    out_ref[0, 1, rows, begin:end] = term_im
+                add(out_ref, (0, 0, rows, slice(begin, end)), sr * fr + si * fi)
+                add(out_ref, (0, 1, rows, slice(begin, end)), si * fr - sr * fi)
             yield
-
-    def run(plan, *parts):
-        for part in plan:
-            next(parts[part], None)
-        for part in parts:
-            for _ in part:
-                pass
-
-    turned = lax.rem(b, 2)
 
     def held(visit):
         z, d = plan[visit]
         d = {"p": 1 + turned, "c": 2 - turned}.get(d, d)
         return z * len(OFFSETS) + d
 
-    def await_visits(*coming):
+    def await_visits(coming):
         for visit in coming:
-            if visit < walkers:
-                arrived(held(visit))
-                z, d = plan[visit]
-                if z and not d:
-                    forward(z)
+            arrived(held(visit))
+            z, d = plan[visit]
+            if z and not d:
+                spread(z)
+            if d == "c":
+                @pl.when(turned == 1)
+                def _(z=z):
+                    relay(z).start()
 
     plan = visits(groups)
-    run((), prepare(0, even))
+    gathers = {}
+
+    def run(ops):
+        for op in ops.split():
+            kind, visit = op[0], int(op[1:])
+            if kind == "T":
+                tabulate(visit)
+            elif kind == "L":
+                lift(visit)
+            else:
+                gathers.setdefault(visit, gather_terms(visit))
+                for _ in gathers[visit]:
+                    if kind == "g":
+                        break
+
     pl.semaphore_wait(barrier, len(peers))
-    for z, d in SENDS:
-        if z < groups:
-            copy(0, order.index((z, d)), place(z, d)).start()
-    run((), gather_terms(even, begun=False))
-    await_visits(1)
-    run((), prepare(held(1), odds))
-    for visit in range(2, walkers, EVERY):
-        await_visits(*range(visit, min(visit + EVERY, walkers)))
-        for coming in range(visit, min(visit + EVERY, walkers)):
-            now, then = (odds, even) if coming % 2 == 0 else (even, odds)
-            run(PLAN, gather_terms(now), prepare(held(coming), then))
-    run((), gather_terms(odds))
-    for slot in range(1, walkers):
-        copy(0, slot, place(1, 0)).wait_send()
+    for z in range(1, groups):
+        if z == 2:
+            spread(0)
+        copy(0, order.index((z, 0)), place(z, 0)).start()
+    if groups == 2:
+        spread(0)
+    run("T0 L0 G0")
+    for coming, ops in blocks(walkers):
+        await_visits(coming)
+        run(ops)
+    for slot, (z, d) in enumerate(order):
+        if slot and d != 3:
+            copy(0, slot, place(1, 0)).wait_send()
+
+    @pl.when(turned == 1)
+    def _():
+        for z in range(groups):
+            copy(0, order.index((z, 3)), place(1, 0)).wait_send()
+            relay(z).wait_send()
 
 
 def local(walker_m, vertex_times, vertex_labels, freq_index, q_index):
@@ -266,10 +309,12 @@
     vmem = pl.BlockSpec(memory_space=pltpu.VMEM)
     smem = pl.BlockSpec(memory_space=pltpu.SMEM)
     bf16 = jnp.bfloat16
-    stage = [
+    table = [
         pltpu.VMEM((2 * v, 2 * v), bf16),
         pltpu.VMEM((2 * v, 2 * v), bf16),
         pltpu.VMEM((held, 2 * v), bf16),
+    ]
+    left = [
         pltpu.VMEM((2 * own, 2 * v), bf16),
         pltpu.VMEM((2 * own, 2 * v), bf16),
     ]
@@ -279,12 +324,13 @@
         in_specs=[vmem, vmem, vmem, smem, smem],
         out_specs=vmem,
         scratch_shapes=[
-            pltpu.VMEM((walkers, v + 16, v), bf16),
+            pltpu.VMEM((walkers, v + 8, v), bf16),
             pltpu.SemaphoreType.DMA((walkers,)),
             pltpu.SemaphoreType.DMA((walkers,)),
+            pltpu.SemaphoreType.DMA((groups,)),
             pltpu.VMEM((nf, v), jnp.int32),
-            *stage,
-            *stage,
+            *table * 3,
+            *left * 2,
         ],
         compiler_params=pltpu.CompilerParams(collective_id=0, has_side_effects=True),
     )(walker_m, vertex_times, vertex_labels, freq_index, q_index)

time: 22 us -> 21.6 us (0.982)
  Pallas kernels: 20 us -> 19.6 us
    pallas_call x1, Pallas kernels: 20 us -> 19.6 us  [local(): pl.pallas_call(functools.partial(kernel, groups, owners), out_shape=pltpu...]
where the time goes in v6:
time: 21.6 us; the launch traced here: 21.4 us
  Pallas kernels  19.6 us (91%)
  local copies, waits for them, and re-layouts  1.14 us (5%)
  between operations  0.66 us (3%)
    pallas_call x1, Pallas kernels, local(): pl.pallas_call(functools.partial(kernel, groups, owners), out_shape=pltpu...  19.6 us
    unnamed x1, local copies, waits for them, and re-layouts  1.14 us

profile of v6, /device:TPU:0, one launch (start us, length us, event | category | flops | bytes accessed | tf_op | source)
XLA Modules:
  0.0 21.4 jit_solution(18146153385137961652)
XLA Ops:
  0.7 19.6 %shard_map.55 = f32[1,2,216,864]{3,2,1,0:T(8,128)S(1)} custom-call(bf16[1,1,128,128]{3,2,1,0:T(8,128)(2,1)} %m_in.1, s32[1,1,128]{2,1,0:T(1,128)} %t_in.1, s32[1,1,128]{2,1,0:T(1,128)} %l_in.1, s32[24]{0:T(128)} %freq_ref.1, s32[1]{0:T(128)S(6)} %copy.8.q_ref), custom_call_target="tpu_custom_call" | custom-call | tf_op jit(solution)/shard_map/pallas_call | solution.py:321
  20.2 1.1 %copy.7 = f32[1,2,216,864]{3,2,1,0:T(8,128)} copy(f32[1,2,216,864]{3,2,1,0:T(8,128)S(1)} %shard_map.55) | data formatting | bytes 2985984
